TPU v7x, 32 devices: a whole 2x2x4 slice. The times are simulated.
32 devices in a mesh: gx: 4 (over y, x), gy: 8 (over z, core).
Axes of the slice: x: 2, y: 2, z: 4, core: 2. Of those that a mesh axis runs over, the one named last changes fastest.
Arguments:
- features: bfloat16 [32, 32, 64, 128], P(None, 'gx', 'gy'), may hold values from -6 to 6
- weight_two: bfloat16 [27, 32, 32], replicated, may hold values from -0.21875 to 0.21875
- bias_two: float32 [32], replicated, may hold values from -3 to 3
- weight_three: bfloat16 [27, 64, 32], replicated, may hold values from -0.21875 to 0.21875
- bias_three: float32 [64], replicated, may hold values from -3 to 3
- weight_four: bfloat16 [27, 128, 64], replicated, may hold values from -0.25 to 0.25
- bias_four: float32 [128], replicated, may hold values from -3 to 3
Outputs:
- level_two: bfloat16 [32, 32, 64, 128], P(None, 'gx', 'gy')
- level_three: bfloat16 [64, 16, 32, 64], P(None, 'gx', 'gy')
- bottleneck: bfloat16 [128, 8, 16, 32], P(None, None, None, 'gy')
All inputs are finite; a program needn't handle non-finite values.
Results may differ from a plain program's by a relative error of at most 0.0085.
Values may be sent and summed in bfloat16 or wider, within the bound.
No kernel may reach another device: no remote copies, remote signals or barrier semaphores. Data moves between devices by JAX's collectives and lax.ppermute only.
A program may use at most 64 MiB of HBM per device.

v0:
```python
import jax
import jax.numpy as jnp
from jax import lax
from jax.sharding import PartitionSpec as P


def extended(cells, sides, width):
    for axis, dim in sides:
        count = lax.axis_size(axis)
        head = lax.slice_in_dim(cells, 0, width, axis=dim)
        tail = lax.slice_in_dim(cells, cells.shape[dim] - width, cells.shape[dim], axis=dim)
        cells = jnp.concatenate(
            [
                lax.ppermute(tail, axis, [(i, (i + 1) % count) for i in range(count)]),
                cells,
                lax.ppermute(head, axis, [((i + 1) % count, i) for i in range(count)]),
            ],
            axis=dim,
        )
    return cells


def wrap_axis(source, axis):
    first = lax.slice_in_dim(source, 0, 1, axis=axis)
    final = lax.slice_in_dim(source, source.shape[axis] - 1, source.shape[axis], axis=axis)
    return jnp.concatenate([final, source, first], axis=axis)


def convolve(padded, weights, bias_values):
    in_channels = padded.shape[0]
    extent_x = padded.shape[1] - 2
    extent_y = padded.shape[2] - 2
    extent_z = padded.shape[3] - 2
    out_channels = weights.shape[1]
    running = jnp.zeros((out_channels, extent_x * extent_y * extent_z), jnp.float32)
    for offset_x in range(3):
        for offset_y in range(3):
            stacked = jnp.concatenate(
                [
                    padded[
                        :,
                        offset_x : offset_x + extent_x,
                        offset_y : offset_y + extent_y,
                        offset_z : offset_z + extent_z,
                    ]
                    for offset_z in range(3)
                ],
                axis=0,
            ).reshape(3 * in_channels, -1)
            first_row = offset_x * 9 + offset_y * 3
            mixing = (
                weights[first_row : first_row + 3]
                .transpose(1, 0, 2)
                .reshape(out_channels, 3 * in_channels)
            )
            running = running + jnp.dot(mixing, stacked, preferred_element_type=jnp.float32)
    result = running + bias_values[:, None]
    result = jax.nn.leaky_relu(result, 0.1).astype(jnp.bfloat16)
    return result.reshape(out_channels, extent_x, extent_y, extent_z)


def average_pool(source):
    channels, extent_x, extent_y, extent_z = source.shape
    blocks = source.astype(jnp.float32).reshape(
        channels, extent_x // 2, 2, extent_y // 2, 2, extent_z // 2, 2
    )
    return blocks.mean(axis=(2, 4, 6)).astype(jnp.bfloat16)


def shards(features, weight_two, bias_two, weight_three, bias_three, weight_four, bias_four):
    rimmed = extended(features, (("gx", 1), ("gy", 2)), 1)
    level_two = convolve(wrap_axis(rimmed, 3), weight_two, bias_two)
    pooled = average_pool(level_two)
    rimmed_three = extended(pooled, (("gx", 1), ("gy", 2)), 1)
    level_three = convolve(wrap_axis(rimmed_three, 3), weight_three, bias_three)
    coarse = average_pool(level_three)
    pieces = lax.all_to_all(coarse, "gy", split_axis=3, concat_axis=2, tiled=True)
    slab_rows = lax.all_gather(pieces, "gx", axis=1, tiled=True)
    deepened = extended(slab_rows, (("gy", 3),), 1)
    padded = wrap_axis(wrap_axis(deepened, 1), 2)
    bottleneck = convolve(padded, weight_four, bias_four)
    return (level_two, level_three, bottleneck)


def solution(mesh):
    return jax.shard_map(
        shards,
        mesh=mesh,
        in_specs=(P(None, "gx", "gy", None), P(), P(), P(), P(), P(), P()),
        out_specs=(P(None, "gx", "gy", None), P(None, "gx", "gy", None), P(None, None, None, "gy")),
        check_vma=False,
    )
```

profile of v0, /device:TPU:0, one launch (start us, length us, event | category | flops | bytes accessed | tf_op | source)
XLA Modules:
  0.0 100.0 jit_solution(3070848087950724654)
XLA Ops:
  0.6 1.5 %copy.174 = bf16[32,8,8,128]{3,0,2,1:T(8,128)(2,1)S(1)} copy(bf16[32,8,8,128]{3,2,1,0:T(8,128)(2,1)} %param.7) | data formatting | bytes 1048576 | tf_op args[0]
  2.1 3.0 %collective-permute-start = (bf16[32,1,8,128]{3,0,2,1:T(8,128)(2,1)S(1)}, bf16[32,1,8,128]{3,0,2,1:T(8,128)(2,1)S(1)}, u32[]{:S(2)}, u32[]{:S(2)}) collective-permute-start(bf16[32,1,8,128]{3,0,2,1:T(8,128)(2,1)S(1)} %get-tuple-element.57), channel_id=1, source_target_pairs={{0,8},{8,16},{16,24},{24,0},{1,9},{9,17},{17,25},{25,1},{2,10},{10... | collective-permute-start | bytes 196616 | tf_op jit(solution)/shard_map/ppermute | solution.py:14
  6.2 2.3 %collective-permute-done = bf16[32,1,8,128]{3,0,2,1:T(8,128)(2,1)S(1)} collective-permute-done((bf16[32,1,8,128]{3,0,2,1:T(8,128)(2,1)S(1)}, bf16[32,1,8,128]{3,0,2,1:T(8,128)(2,1)S(1)}, u32[]{:S(2)}, u32[]{:S(2)}) %collective-permute-start) | collective-permute-done | bytes 65568 | tf_op jit(solution)/shard_map/ppermute | solution.py:14
  9.9 2.2 %collective-permute-start.3 = (bf16[32,10,1,128]{3,0,2,1:T(8,128)(2,1)S(1)}, bf16[32,10,1,128]{3,0,2,1:T(8,128)(2,1)S(1)}, u32[]{:S(2)}, u32[]{:S(2)}) collective-permute-start(bf16[32,10,1,128]{3,0,2,1:T(8,128)(2,1)S(1)} %get-tuple-element.52), channel_id=1, source_target_pairs={{1,0},{2,1},{3,2},{4,3},{5,4},{6,5},{7,6},{0,7},{9,8},{10,9},{11,1... | collective-permute-start | bytes 245768 | tf_op jit(solution)/shard_map/ppermute | solution.py:16
  14.2 3.6 %collective-permute-done.2 = bf16[32,10,1,128]{3,0,2,1:T(8,128)(2,1)S(1)} collective-permute-done((bf16[32,10,1,128]{3,0,2,1:T(8,128)(2,1)S(1)}, bf16[32,10,1,128]{3,0,2,1:T(8,128)(2,1)S(1)}, u32[]{:S(2)}, u32[]{:S(2)}) %collective-permute-start.2) | collective-permute-done | bytes 81952 | tf_op jit(solution)/shard_map/ppermute | solution.py:14
  18.2 1.7 %maximum_maximum_fusion = (bf16[32,10,10,129]{3,0,2,1:T(8,128)(2,1)S(1)}, bf16[32,10,10,129]{3,0,2,1:T(8,128)(2,1)S(1)}) fusion(bf16[32,10,1,128]{3,0,2,1:T(8,128)(2,1)S(1)} %collective-permute-done.3, bf16[32,10,8,128]{3,0,2,1:T(8,128)(2,1)S(1)} %constant_dynamic-update-slice_fusion, bf16[32,10,1,128]{3,0,2,1:T(8,128)(2,1)S(1)} %collective-permute-done.2, ...), kind=kLoop, calls=%fused_computation.11 | loop fusion | flops 6604800 | bytes 2483200 | tf_op jit(solution)/shard_map/concatenate | solution.py:26
  19.9 2.8 %fusion.60 = (bf16[32,8,8,128]{3,0,2,1:T(8,128)(2,1)S(1)}, bf16[32,8,8,128]{3,0,2,1:T(8,128)(2,1)S(1)}, bf16[32,8,8,128]{3,0,2,1:T(8,128)(2,1)S(1)}, bf16[32,8,8...) fusion(bf16[32,10,10,129]{3,0,2,1:T(8,128)(2,1)S(1)} %get-tuple, ...), kind=kLoop, calls=%fused_computation.164 | loop fusion | bytes 18874368 | tf_op jit(solution)/shard_map/slice | solution.py:40
  31.1 1.1 %convolution_add_fusion.7 = f32[8192,32]{0,1:T(8,128)S(1)} fusion(f32[8192,32]{0,1:T(8,128)S(1)} %fusion.18, bf16[32,96]{1,0:T(8,128)(2,1)S(1)} %reshape.191, bf16[12,8,64,128]{3,2,1,0:T(8,128)(2,1)S(1)} %bitcast.227), kind=kOutput, calls=%fused_computation.9 | convolution fusion | flops 50593792 | bytes 3676160 | tf_op jit(solution)/shard_map/dot_general | solution.py:56
  33.4 1.1 %convolution_add_fusion.5 = f32[8192,32]{0,1:T(8,128)S(1)} fusion(f32[8192,32]{0,1:T(8,128)S(1)} %convolution_add_fusion.6, bf16[32,96]{1,0:T(8,128)(2,1)S(1)} %reshape.195, bf16[12,8,64,128]{3,2,1,0:T(8,128)(2,1)S(1)} %bitcast.230), kind=kOutput, calls=%fused_computation.7 | convolution fusion | flops 50593792 | bytes 3676160 | tf_op jit(solution)/shard_map/dot_general | solution.py:56
  34.5 1.1 %convolution_add_fusion.4 = f32[8192,32]{0,1:T(8,128)S(1)} fusion(f32[8192,32]{0,1:T(8,128)S(1)} %convolution_add_fusion.5, bf16[32,96]{1,0:T(8,128)(2,1)S(1)} %reshape.197, bf16[12,8,64,128]{3,2,1,0:T(8,128)(2,1)S(1)} %bitcast.229), kind=kOutput, calls=%fused_computation.6 | convolution fusion | flops 50593792 | bytes 3676160 | tf_op jit(solution)/shard_map/dot_general | solution.py:56
  36.7 1.1 %convolution_add_fusion.2 = f32[8192,32]{0,1:T(8,128)S(1)} fusion(f32[8192,32]{0,1:T(8,128)S(1)} %convolution_add_fusion.3, bf16[32,96]{1,0:T(8,128)(2,1)S(1)} %reshape.201, bf16[12,8,64,128]{3,2,1,0:T(8,128)(2,1)S(1)} %bitcast.233), kind=kOutput, calls=%fused_computation.4 | convolution fusion | flops 50593792 | bytes 3676160 | tf_op jit(solution)/shard_map/dot_general | solution.py:56
  37.9 1.1 %convolution_add_fusion.1 = f32[8192,32]{0,1:T(8,128)S(1)} fusion(f32[8192,32]{0,1:T(8,128)S(1)} %convolution_add_fusion.2, bf16[32,96]{1,0:T(8,128)(2,1)S(1)} %reshape.203, bf16[12,8,64,128]{3,2,1,0:T(8,128)(2,1)S(1)} %bitcast.232), kind=kOutput, calls=%fused_computation.3 | convolution fusion | flops 50593792 | bytes 3676160 | tf_op jit(solution)/shard_map/dot_general | solution.py:56
  39.0 1.1 %fusion.31 = bf16[32,8192]{1,0:T(8,128)(2,1)S(1)} fusion(f32[8192,32]{0,1:T(8,128)S(1)} %convolution_add_fusion.1, bf16[32,96]{1,0:T(8,128)(2,1)S(1)} %reshape.205, bf16[12,8,64,128]{3,2,1,0:T(8,128)(2,1)S(1)} %bitcast.234, f32[32]{0:T(128)S(1)} %copy-done.13), kind=kOutput, calls=%fused_computation.49 | convolution fusion | flops 51904512 | bytes 3152000 | tf_op jit(solution)/shard_map/dot_general | solution.py:56
  40.1 2.4 %copy.198 = f32[32,8192]{0,1:T(8,128)} copy(bf16[32,8192]{1,0:T(8,128)(2,1)S(1)} %fusion.31) | data formatting | bytes 1572864 | tf_op jit(solution)/shard_map/convert_element_type | solution.py:64
  42.5 4.8 %reduce_sum.18 = f32[32,4,4,64]{0,3,2,1:T(8,128)S(1)} reduce(f32[32,4,2,4,2,64,2]{0,6,5,4,3,2,1:T(2,128)} %bitcast.225, f32[]{:T(128)} %constant.6.clone.1), dimensions={2,4,6}, to_apply=%region_0.1 | reduce | flops 229376 | bytes 1179652 | tf_op jit(solution)/shard_map/reduce_sum | solution.py:67
  47.4 2.1 %collective-permute-start.5 = (bf16[32,1,4,64]{0,3,2,1:T(8,128)(2,1)S(1)}, bf16[32,1,4,64]{0,3,2,1:T(8,128)(2,1)S(1)}, u32[]{:S(2)}, u32[]{:S(2)}) collective-permute-start(bf16[32,1,4,64]{0,3,2,1:T(8,128)(2,1)S(1)} %get-tuple-element.99), channel_id=1, source_target_pairs={{8,0},{16,8},{24,16},{0,24},{9,1},{17,9},{25,17},{1,25},{10,2},{18... | collective-permute-start | bytes 49160 | tf_op jit(solution)/shard_map/ppermute | solution.py:16
  49.6 2.2 %collective-permute-done.5 = bf16[32,1,4,64]{0,3,2,1:T(8,128)(2,1)S(1)} collective-permute-done((bf16[32,1,4,64]{0,3,2,1:T(8,128)(2,1)S(1)}, bf16[32,1,4,64]{0,3,2,1:T(8,128)(2,1)S(1)}, u32[]{:S(2)}, u32[]{:S(2)}) %collective-permute-start.5) | collective-permute-done | bytes 16416 | tf_op jit(solution)/shard_map/ppermute | solution.py:16
  51.8 2.9 %collective-permute-done.4 = bf16[32,1,4,64]{0,3,2,1:T(8,128)(2,1)S(1)} collective-permute-done((bf16[32,1,4,64]{0,3,2,1:T(8,128)(2,1)S(1)}, bf16[32,1,4,64]{0,3,2,1:T(8,128)(2,1)S(1)}, u32[]{:S(2)}, u32[]{:S(2)}) %collective-permute-start.4) | collective-permute-done | bytes 16416 | tf_op jit(solution)/shard_map/ppermute | solution.py:14
  55.3 2.5 %collective-permute-done.7 = bf16[32,6,1,64]{0,3,2,1:T(8,128)(2,1)S(1)} collective-permute-done((bf16[32,6,1,64]{0,3,2,1:T(8,128)(2,1)S(1)}, bf16[32,6,1,64]{0,3,2,1:T(8,128)(2,1)S(1)}, u32[]{:S(2)}, u32[]{:S(2)}) %collective-permute-start.7) | collective-permute-done | bytes 24608 | tf_op jit(solution)/shard_map/ppermute | solution.py:16
  57.8 2.9 %collective-permute-done.6 = bf16[32,6,1,64]{0,3,2,1:T(8,128)(2,1)S(1)} collective-permute-done((bf16[32,6,1,64]{0,3,2,1:T(8,128)(2,1)S(1)}, bf16[32,6,1,64]{0,3,2,1:T(8,128)(2,1)S(1)}, u32[]{:S(2)}, u32[]{:S(2)}) %collective-permute-start.6) | collective-permute-done | bytes 24608 | tf_op jit(solution)/shard_map/ppermute | solution.py:14
  67.9 8.0 %all_to_all.18 = bf16[8,2,512]{2,1,0:T(2,128)(2,1)S(1)} all-to-all(bf16[8,2,512]{2,1,0:T(2,128)(2,1)S(1)} %reshape.247), channel_id=1, replica_groups=mesh['gx'=4,'gy'=8] {'gy'}, dimensions={0} | all-to-all | bytes 32768 | tf_op jit(solution)/shard_map/all_to_all | solution.py:77
  76.0 8.5 %all_gather.3 = bf16[64,8,16,4]{0,2,3,1:T(8,128)(2,1)S(1)} all-gather(bf16[64,2,16,4]{0,2,3,1:T(8,128)(2,1)S(1)} %bitcast.257), channel_id=1, replica_groups=mesh['gx'=4,'gy'=8] {'gx'}, dimensions={1}, use_global_device_ids=true | all-gather | bytes 81920 | tf_op jit(solution)/shard_map/all_gather | solution.py:78
  87.1 3.5 %collective-permute-start.9 = (bf16[64,8,16,1]{0,2,3,1:T(8,128)(2,1)S(1)}, bf16[64,8,16,1]{0,2,3,1:T(8,128)(2,1)S(1)}, u32[]{:S(2)}, u32[]{:S(2)}) collective-permute-start(bf16[64,8,16,1]{0,2,3,1:T(8,128)(2,1)S(1)} %get-tuple-element.130), channel_id=1, source_target_pairs={{1,0},{2,1},{3,2},{4,3},{5,4},{6,5},{7,6},{0,7},{9,8},{10,9},{11,1... | collective-permute-start | bytes 49160 | tf_op jit(solution)/shard_map/ppermute | solution.py:16
  90.7 1.6 %collective-permute-done.9 = bf16[64,8,16,1]{0,2,3,1:T(8,128)(2,1)S(1)} collective-permute-done((bf16[64,8,16,1]{0,2,3,1:T(8,128)(2,1)S(1)}, bf16[64,8,16,1]{0,2,3,1:T(8,128)(2,1)S(1)}, u32[]{:S(2)}, u32[]{:S(2)}) %collective-permute-start.9) | collective-permute-done | bytes 16416 | tf_op jit(solution)/shard_map/ppermute | solution.py:16
  (164 shorter events, 33.3 us)
Async XLA Ops:
  0.6 7.8 %copy-start = (bf16[32,8,8,128]{3,2,1,0:T(8,128)(2,1)S(1)}, bf16[32,8,8,128]{3,2,1,0:T(8,128)(2,1)}, u32[]{:S(2)}) copy-start(bf16[32,8,8,128]{3,2,1,0:T(8,128)(2,1)} %param.7) | copy-start | bytes 1572868
  0.6 11.5 %copy-start.2 = (bf16[27,32,32]{2,1,0:T(8,128)(2,1)S(1)}, bf16[27,32,32]{2,1,0:T(8,128)(2,1)}, u32[]{:S(2)}) copy-start(bf16[27,32,32]{2,1,0:T(8,128)(2,1)} %param.8) | copy-start | bytes 165892
  2.1 6.3 %collective-permute-start = (bf16[32,1,8,128]{3,0,2,1:T(8,128)(2,1)S(1)}, bf16[32,1,8,128]{3,0,2,1:T(8,128)(2,1)S(1)}, u32[]{:S(2)}, u32[]{:S(2)}) collective-permute-start(bf16[32,1,8,128]{3,0,2,1:T(8,128)(2,1)S(1)} %get-tuple-element.57), channel_id=1, source_target_pairs={{0,8},{8,16},{16,24},{24,0},{1,9},{9,17},{17,25},{25,1},{2,10},{10... | collective-permute-start | bytes 196616 | tf_op jit(solution)/shard_map/ppermute | solution.py:14
  5.1 4.7 %collective-permute-start.1 = (bf16[32,1,8,128]{3,0,2,1:T(8,128)(2,1)S(1)}, bf16[32,1,8,128]{3,0,2,1:T(8,128)(2,1)S(1)}, u32[]{:S(2)}, u32[]{:S(2)}) collective-permute-start(bf16[32,1,8,128]{3,0,2,1:T(8,128)(2,1)S(1)} %get-tuple-element.56), channel_id=1, source_target_pairs={{8,0},{16,8},{24,16},{0,24},{9,1},{17,9},{25,17},{1,25},{10,2},{18... | collective-permute-start | bytes 196616 | tf_op jit(solution)/shard_map/ppermute | solution.py:16
  9.9 4.3 %collective-permute-start.3 = (bf16[32,10,1,128]{3,0,2,1:T(8,128)(2,1)S(1)}, bf16[32,10,1,128]{3,0,2,1:T(8,128)(2,1)S(1)}, u32[]{:S(2)}, u32[]{:S(2)}) collective-permute-start(bf16[32,10,1,128]{3,0,2,1:T(8,128)(2,1)S(1)} %get-tuple-element.52), channel_id=1, source_target_pairs={{1,0},{2,1},{3,2},{4,3},{5,4},{6,5},{7,6},{0,7},{9,8},{10,9},{11,1... | collective-permute-start | bytes 245768 | tf_op jit(solution)/shard_map/ppermute | solution.py:16
  12.1 5.7 %collective-permute-start.2 = (bf16[32,10,1,128]{3,0,2,1:T(8,128)(2,1)S(1)}, bf16[32,10,1,128]{3,0,2,1:T(8,128)(2,1)S(1)}, u32[]{:S(2)}, u32[]{:S(2)}) collective-permute-start(bf16[32,10,1,128]{3,0,2,1:T(8,128)(2,1)S(1)} %get-tuple-element.51), channel_id=1, source_target_pairs={{0,1},{1,2},{2,3},{3,4},{4,5},{5,6},{6,7},{7,0},{8,9},{9,10},{10,1... | collective-permute-start | bytes 245768 | tf_op jit(solution)/shard_map/ppermute | solution.py:14
  37.8 1.1 %copy-start.13 = (f32[32]{0:T(128)S(1)}, f32[32]{0:T(128)}, u32[]{:S(2)}) copy-start(f32[32]{0:T(128)} %param.9) | copy-start | bytes 388
  47.3 7.9 %copy-start.3 = (bf16[27,64,32]{1,2,0:T(8,128)(2,1)S(1)}, bf16[27,64,32]{1,2,0:T(8,128)(2,1)}, u32[]{:S(2)}) copy-start(bf16[27,64,32]{1,2,0:T(8,128)(2,1)} %param.10) | copy-start | bytes 331780
  47.4 4.4 %collective-permute-start.5 = (bf16[32,1,4,64]{0,3,2,1:T(8,128)(2,1)S(1)}, bf16[32,1,4,64]{0,3,2,1:T(8,128)(2,1)S(1)}, u32[]{:S(2)}, u32[]{:S(2)}) collective-permute-start(bf16[32,1,4,64]{0,3,2,1:T(8,128)(2,1)S(1)} %get-tuple-element.99), channel_id=1, source_target_pairs={{8,0},{16,8},{24,16},{0,24},{9,1},{17,9},{25,17},{1,25},{10,2},{18... | collective-permute-start | bytes 49160 | tf_op jit(solution)/shard_map/ppermute | solution.py:16
  49.5 5.2 %collective-permute-start.4 = (bf16[32,1,4,64]{0,3,2,1:T(8,128)(2,1)S(1)}, bf16[32,1,4,64]{0,3,2,1:T(8,128)(2,1)S(1)}, u32[]{:S(2)}, u32[]{:S(2)}) collective-permute-start(bf16[32,1,4,64]{0,3,2,1:T(8,128)(2,1)S(1)} %get-tuple-element.98), channel_id=1, source_target_pairs={{0,8},{8,16},{16,24},{24,0},{1,9},{9,17},{17,25},{25,1},{2,10},{10... | collective-permute-start | bytes 49160 | tf_op jit(solution)/shard_map/ppermute | solution.py:14
  54.7 3.1 %collective-permute-start.7 = (bf16[32,6,1,64]{0,3,2,1:T(8,128)(2,1)S(1)}, bf16[32,6,1,64]{0,3,2,1:T(8,128)(2,1)S(1)}, u32[]{:S(2)}, u32[]{:S(2)}) collective-permute-start(bf16[32,6,1,64]{0,3,2,1:T(8,128)(2,1)S(1)} %get-tuple-element.76), channel_id=1, source_target_pairs={{1,0},{2,1},{3,2},{4,3},{5,4},{6,5},{7,6},{0,7},{9,8},{10,9},{11,1... | collective-permute-start | bytes 73736 | tf_op jit(solution)/shard_map/ppermute | solution.py:16
  54.8 5.9 %collective-permute-start.6 = (bf16[32,6,1,64]{0,3,2,1:T(8,128)(2,1)S(1)}, bf16[32,6,1,64]{0,3,2,1:T(8,128)(2,1)S(1)}, u32[]{:S(2)}, u32[]{:S(2)}) collective-permute-start(bf16[32,6,1,64]{0,3,2,1:T(8,128)(2,1)S(1)} %get-tuple-element.75), channel_id=1, source_target_pairs={{0,1},{1,2},{2,3},{3,4},{4,5},{5,6},{6,7},{7,0},{8,9},{9,10},{10,1... | collective-permute-start | bytes 73736 | tf_op jit(solution)/shard_map/ppermute | solution.py:14
  66.2 0.8 copy-start.11
  67.0 17.6 %copy-start.1 = (bf16[27,128,64]{1,2,0:T(8,128)(2,1)S(1)}, bf16[27,128,64]{1,2,0:T(8,128)(2,1)}, u32[]{:S(2)}) copy-start(bf16[27,128,64]{1,2,0:T(8,128)(2,1)} %param.12) | copy-start | bytes 1327108
  84.5 6.1 %collective-permute-start.8 = (bf16[64,8,16,1]{0,2,3,1:T(8,128)(2,1)S(1)}, bf16[64,8,16,1]{0,2,3,1:T(8,128)(2,1)S(1)}, u32[]{:S(2)}, u32[]{:S(2)}) collective-permute-start(bf16[64,8,16,1]{0,2,3,1:T(8,128)(2,1)S(1)} %get-tuple-element.131), channel_id=1, source_target_pairs={{0,1},{1,2},{2,3},{3,4},{4,5},{5,6},{6,7},{7,0},{8,9},{9,10},{10,1... | collective-permute-start | bytes 49160 | tf_op jit(solution)/shard_map/ppermute | solution.py:14
  87.1 5.1 %collective-permute-start.9 = (bf16[64,8,16,1]{0,2,3,1:T(8,128)(2,1)S(1)}, bf16[64,8,16,1]{0,2,3,1:T(8,128)(2,1)S(1)}, u32[]{:S(2)}, u32[]{:S(2)}) collective-permute-start(bf16[64,8,16,1]{0,2,3,1:T(8,128)(2,1)S(1)} %get-tuple-element.130), channel_id=1, source_target_pairs={{1,0},{2,1},{3,2},{4,3},{5,4},{6,5},{7,6},{0,7},{9,8},{10,9},{11,1... | collective-permute-start | bytes 49160 | tf_op jit(solution)/shard_map/ppermute | solution.py:16
  92.2 0.6 copy-start.9
  94.2 0.9 copy-start.10
  96.3 1.0 copy-start.8
  96.5 1.0 %copy-start.7 = (bf16[3,128,64]{1,2,0:T(8,128)(2,1)S(1)}, bf16[3,128,64]{1,2,0:T(8,128)(2,1)}, u32[]{:S(2)}) copy-start(bf16[3,128,64]{1,2,0:T(8,128)(2,1)} %get-tuple-element.70) | copy-start | bytes 147460
  96.8 0.9 copy-start.6
  97.0 1.0 %copy-start.5 = (bf16[3,128,64]{1,2,0:T(8,128)(2,1)S(1)}, bf16[3,128,64]{1,2,0:T(8,128)(2,1)}, u32[]{:S(2)}) copy-start(bf16[3,128,64]{1,2,0:T(8,128)(2,1)} %get-tuple-element.68) | copy-start | bytes 147460
  97.3 0.9 copy-start.4
  98.2 0.9 copy-start.12
where the time goes:
time: 100 us
  local copies, waits for them, and re-layouts  21.7 us (22%)
  waiting for transfers between devices  19.9 us (20%)
  blocking collectives  16.5 us (16%)
  matrix products  14.8 us (15%)
  other arithmetic  12.9 us (13%)
  starting transfers between devices  12.6 us (13%)
  between operations  1.59 us (2%)
    dot_general x27, matrix products, convolve(): jnp.dot(mixing, stacked, preferred_element_type=jnp.float32)  14.8 us
    ppermute x5, waiting for transfers between devices, extended(): lax.ppermute(tail, axis, [(i, (i + 1) % count) for i in range(count)])  11.6 us
    ppermute x5, starting transfers between devices, extended(): lax.ppermute(head, axis, [((i + 1) % count, i) for i in range(count)])  8.9 us
    all_gather x1, blocking collectives, shards(): slab_rows = lax.all_gather(pieces, 'gx', axis=1, tiled=True)  8.49 us
    ppermute x5, waiting for transfers between devices, extended(): lax.ppermute(head, axis, [((i + 1) % count, i) for i in range(count)])  8.26 us
    all_to_all x1, blocking collectives, shards(): lax.all_to_all(coarse, 'gy', split_axis=3, concat_axis=2, tiled=True)  8.02 us
    concatenate x18, local copies, waits for them, and re-layouts, convolve(): jnp.concatenate([padded[:, offset_x:offset_x + extent_x, offset_y:offset_...  6.73 us
    reduce_sum x2, other arithmetic, average_pool(): return blocks.mean(axis=(2, 4, 6)).astype(jnp.bfloat16)  5.15 us
  transfers between devices with their start and end apart: 10, of which 9 were waited for; matrix products, arithmetic and copies ran while one was open for 4% of the time, Pallas kernels for 0%

commit v1 on v0

--- a/solution.py
+++ b/solution.py
@@ -74,7 +74,10 @@
     rimmed_three = extended(pooled, (("gx", 1), ("gy", 2)), 1)
     level_three = convolve(wrap_axis(rimmed_three, 3), weight_three, bias_three)
     coarse = average_pool(level_three)
-    pieces = lax.all_to_all(coarse, "gy", split_axis=3, concat_axis=2, tiled=True)
+    count_2 = lax.axis_size("gy")
+    parts = jnp.stack(jnp.split(coarse, count_2, axis=3), axis=0)
+    parts = lax.all_to_all(parts, "gy", split_axis=0, concat_axis=0)
+    pieces = jnp.concatenate(parts, axis=2)
     slab_rows = lax.all_gather(pieces, "gx", axis=1, tiled=True)
     deepened = extended(slab_rows, (("gy", 3),), 1)
     padded = wrap_axis(wrap_axis(deepened, 1), 2)

time: 100 us -> 100 us (level)
    unnamed x36 -> x43, local copies, waits for them, and re-layouts: 3.16 us -> 3.24 us
where the time goes in v1:
time: 100 us
  local copies, waits for them, and re-layouts  21.8 us (22%)
  waiting for transfers between devices  19.9 us (20%)
  blocking collectives  16.5 us (16%)
  matrix products  14.8 us (15%)
  other arithmetic  12.9 us (13%)
  starting transfers between devices  12.6 us (13%)
  between operations  1.62 us (2%)
    dot_general x27, matrix products, convolve(): jnp.dot(mixing, stacked, preferred_element_type=jnp.float32)  14.8 us
    ppermute x5, waiting for transfers between devices, extended(): lax.ppermute(tail, axis, [(i, (i + 1) % count) for i in range(count)])  11.6 us
    ppermute x5, starting transfers between devices, extended(): lax.ppermute(head, axis, [((i + 1) % count, i) for i in range(count)])  8.9 us
    all_gather x1, blocking collectives, shards(): slab_rows = lax.all_gather(pieces, 'gx', axis=1, tiled=True)  8.49 us
    ppermute x5, waiting for transfers between devices, extended(): lax.ppermute(head, axis, [((i + 1) % count, i) for i in range(count)])  8.26 us
    all_to_all x1, blocking collectives, shards(): parts = lax.all_to_all(parts, 'gy', split_axis=0, concat_axis=0)  8.02 us
    concatenate x18, local copies, waits for them, and re-layouts, convolve(): jnp.concatenate([padded[:, offset_x:offset_x + extent_x, offset_y:offset_...  6.73 us
    reduce_sum x2, other arithmetic, average_pool(): return blocks.mean(axis=(2, 4, 6)).astype(jnp.bfloat16)  5.15 us
  transfers between devices with their start and end apart: 10, of which 9 were waited for; matrix products, arithmetic and copies ran while one was open for 4% of the time, Pallas kernels for 0%

profile of v1, /device:TPU:0, one launch (start us, length us, event | category | flops | bytes accessed | tf_op | source)
XLA Modules:
  0.0 100.2 jit_solution(5755542956501353951)
XLA Ops:
  0.6 1.5 %copy.179 = bf16[32,8,8,128]{3,0,2,1:T(8,128)(2,1)S(1)} copy(bf16[32,8,8,128]{3,2,1,0:T(8,128)(2,1)} %param.7) | data formatting | bytes 1048576 | tf_op args[0]
  2.1 3.0 %collective-permute-start = (bf16[32,1,8,128]{3,0,2,1:T(8,128)(2,1)S(1)}, bf16[32,1,8,128]{3,0,2,1:T(8,128)(2,1)S(1)}, u32[]{:S(2)}, u32[]{:S(2)}) collective-permute-start(bf16[32,1,8,128]{3,0,2,1:T(8,128)(2,1)S(1)} %get-tuple-element.57), channel_id=1, source_target_pairs={{0,8},{8,16},{16,24},{24,0},{1,9},{9,17},{17,25},{25,1},{2,10},{10... | collective-permute-start | bytes 196616 | tf_op jit(solution)/shard_map/ppermute | solution.py:14
  6.2 2.3 %collective-permute-done = bf16[32,1,8,128]{3,0,2,1:T(8,128)(2,1)S(1)} collective-permute-done((bf16[32,1,8,128]{3,0,2,1:T(8,128)(2,1)S(1)}, bf16[32,1,8,128]{3,0,2,1:T(8,128)(2,1)S(1)}, u32[]{:S(2)}, u32[]{:S(2)}) %collective-permute-start) | collective-permute-done | bytes 65568 | tf_op jit(solution)/shard_map/ppermute | solution.py:14
  9.9 2.2 %collective-permute-start.3 = (bf16[32,10,1,128]{3,0,2,1:T(8,128)(2,1)S(1)}, bf16[32,10,1,128]{3,0,2,1:T(8,128)(2,1)S(1)}, u32[]{:S(2)}, u32[]{:S(2)}) collective-permute-start(bf16[32,10,1,128]{3,0,2,1:T(8,128)(2,1)S(1)} %get-tuple-element.52), channel_id=1, source_target_pairs={{1,0},{2,1},{3,2},{4,3},{5,4},{6,5},{7,6},{0,7},{9,8},{10,9},{11,1... | collective-permute-start | bytes 245768 | tf_op jit(solution)/shard_map/ppermute | solution.py:16
  14.2 3.6 %collective-permute-done.2 = bf16[32,10,1,128]{3,0,2,1:T(8,128)(2,1)S(1)} collective-permute-done((bf16[32,10,1,128]{3,0,2,1:T(8,128)(2,1)S(1)}, bf16[32,10,1,128]{3,0,2,1:T(8,128)(2,1)S(1)}, u32[]{:S(2)}, u32[]{:S(2)}) %collective-permute-start.2) | collective-permute-done | bytes 81952 | tf_op jit(solution)/shard_map/ppermute | solution.py:14
  18.2 1.7 %maximum_maximum_fusion = (bf16[32,10,10,129]{3,0,2,1:T(8,128)(2,1)S(1)}, bf16[32,10,10,129]{3,0,2,1:T(8,128)(2,1)S(1)}) fusion(bf16[32,10,1,128]{3,0,2,1:T(8,128)(2,1)S(1)} %collective-permute-done.3, bf16[32,10,8,128]{3,0,2,1:T(8,128)(2,1)S(1)} %constant_dynamic-update-slice_fusion, bf16[32,10,1,128]{3,0,2,1:T(8,128)(2,1)S(1)} %collective-permute-done.2, ...), kind=kLoop, calls=%fused_computation.11 | loop fusion | flops 6604800 | bytes 2483200 | tf_op jit(solution)/shard_map/concatenate | solution.py:26
  19.9 2.8 %fusion.60 = (bf16[32,8,8,128]{3,0,2,1:T(8,128)(2,1)S(1)}, bf16[32,8,8,128]{3,0,2,1:T(8,128)(2,1)S(1)}, bf16[32,8,8,128]{3,0,2,1:T(8,128)(2,1)S(1)}, bf16[32,8,8...) fusion(bf16[32,10,10,129]{3,0,2,1:T(8,128)(2,1)S(1)} %get-tuple, ...), kind=kLoop, calls=%fused_computation.180 | loop fusion | bytes 18874368 | tf_op jit(solution)/shard_map/slice | solution.py:40
  31.1 1.1 %convolution_add_fusion.7 = f32[8192,32]{0,1:T(8,128)S(1)} fusion(f32[8192,32]{0,1:T(8,128)S(1)} %fusion.18, bf16[32,96]{1,0:T(8,128)(2,1)S(1)} %reshape.197, bf16[12,8,64,128]{3,2,1,0:T(8,128)(2,1)S(1)} %bitcast.259), kind=kOutput, calls=%fused_computation.9 | convolution fusion | flops 50593792 | bytes 3676160 | tf_op jit(solution)/shard_map/dot_general | solution.py:56
  33.4 1.1 %convolution_add_fusion.5 = f32[8192,32]{0,1:T(8,128)S(1)} fusion(f32[8192,32]{0,1:T(8,128)S(1)} %convolution_add_fusion.6, bf16[32,96]{1,0:T(8,128)(2,1)S(1)} %reshape.201, bf16[12,8,64,128]{3,2,1,0:T(8,128)(2,1)S(1)} %bitcast.262), kind=kOutput, calls=%fused_computation.7 | convolution fusion | flops 50593792 | bytes 3676160 | tf_op jit(solution)/shard_map/dot_general | solution.py:56
  34.5 1.1 %convolution_add_fusion.4 = f32[8192,32]{0,1:T(8,128)S(1)} fusion(f32[8192,32]{0,1:T(8,128)S(1)} %convolution_add_fusion.5, bf16[32,96]{1,0:T(8,128)(2,1)S(1)} %reshape.203, bf16[12,8,64,128]{3,2,1,0:T(8,128)(2,1)S(1)} %bitcast.261), kind=kOutput, calls=%fused_computation.6 | convolution fusion | flops 50593792 | bytes 3676160 | tf_op jit(solution)/shard_map/dot_general | solution.py:56
  36.7 1.1 %convolution_add_fusion.2 = f32[8192,32]{0,1:T(8,128)S(1)} fusion(f32[8192,32]{0,1:T(8,128)S(1)} %convolution_add_fusion.3, bf16[32,96]{1,0:T(8,128)(2,1)S(1)} %reshape.207, bf16[12,8,64,128]{3,2,1,0:T(8,128)(2,1)S(1)} %bitcast.265), kind=kOutput, calls=%fused_computation.4 | convolution fusion | flops 50593792 | bytes 3676160 | tf_op jit(solution)/shard_map/dot_general | solution.py:56
  37.9 1.1 %convolution_add_fusion.1 = f32[8192,32]{0,1:T(8,128)S(1)} fusion(f32[8192,32]{0,1:T(8,128)S(1)} %convolution_add_fusion.2, bf16[32,96]{1,0:T(8,128)(2,1)S(1)} %reshape.209, bf16[12,8,64,128]{3,2,1,0:T(8,128)(2,1)S(1)} %bitcast.264), kind=kOutput, calls=%fused_computation.3 | convolution fusion | flops 50593792 | bytes 3676160 | tf_op jit(solution)/shard_map/dot_general | solution.py:56
  39.0 1.1 %fusion.31 = bf16[32,8192]{1,0:T(8,128)(2,1)S(1)} fusion(f32[8192,32]{0,1:T(8,128)S(1)} %convolution_add_fusion.1, bf16[32,96]{1,0:T(8,128)(2,1)S(1)} %reshape.211, bf16[12,8,64,128]{3,2,1,0:T(8,128)(2,1)S(1)} %bitcast.266, f32[32]{0:T(128)S(1)} %copy-done.13), kind=kOutput, calls=%fused_computation.49 | convolution fusion | flops 51904512 | bytes 3152000 | tf_op jit(solution)/shard_map/dot_general | solution.py:56
  40.1 2.4 %copy.203 = f32[32,8192]{0,1:T(8,128)} copy(bf16[32,8192]{1,0:T(8,128)(2,1)S(1)} %fusion.31) | data formatting | bytes 1572864 | tf_op jit(solution)/shard_map/convert_element_type | solution.py:64
  42.5 4.8 %reduce_sum.18 = f32[32,4,4,64]{0,3,2,1:T(8,128)S(1)} reduce(f32[32,4,2,4,2,64,2]{0,6,5,4,3,2,1:T(2,128)} %bitcast.257, f32[]{:T(128)} %constant.6.clone.1), dimensions={2,4,6}, to_apply=%region_0.1 | reduce | flops 229376 | bytes 1179652 | tf_op jit(solution)/shard_map/reduce_sum | solution.py:67
  47.4 2.1 %collective-permute-start.5 = (bf16[32,1,4,64]{0,3,2,1:T(8,128)(2,1)S(1)}, bf16[32,1,4,64]{0,3,2,1:T(8,128)(2,1)S(1)}, u32[]{:S(2)}, u32[]{:S(2)}) collective-permute-start(bf16[32,1,4,64]{0,3,2,1:T(8,128)(2,1)S(1)} %get-tuple-element.99), channel_id=1, source_target_pairs={{8,0},{16,8},{24,16},{0,24},{9,1},{17,9},{25,17},{1,25},{10,2},{18... | collective-permute-start | bytes 49160 | tf_op jit(solution)/shard_map/ppermute | solution.py:16
  49.6 2.2 %collective-permute-done.5 = bf16[32,1,4,64]{0,3,2,1:T(8,128)(2,1)S(1)} collective-permute-done((bf16[32,1,4,64]{0,3,2,1:T(8,128)(2,1)S(1)}, bf16[32,1,4,64]{0,3,2,1:T(8,128)(2,1)S(1)}, u32[]{:S(2)}, u32[]{:S(2)}) %collective-permute-start.5) | collective-permute-done | bytes 16416 | tf_op jit(solution)/shard_map/ppermute | solution.py:16
  51.8 2.9 %collective-permute-done.4 = bf16[32,1,4,64]{0,3,2,1:T(8,128)(2,1)S(1)} collective-permute-done((bf16[32,1,4,64]{0,3,2,1:T(8,128)(2,1)S(1)}, bf16[32,1,4,64]{0,3,2,1:T(8,128)(2,1)S(1)}, u32[]{:S(2)}, u32[]{:S(2)}) %collective-permute-start.4) | collective-permute-done | bytes 16416 | tf_op jit(solution)/shard_map/ppermute | solution.py:14
  55.3 2.5 %collective-permute-done.7 = bf16[32,6,1,64]{0,3,2,1:T(8,128)(2,1)S(1)} collective-permute-done((bf16[32,6,1,64]{0,3,2,1:T(8,128)(2,1)S(1)}, bf16[32,6,1,64]{0,3,2,1:T(8,128)(2,1)S(1)}, u32[]{:S(2)}, u32[]{:S(2)}) %collective-permute-start.7) | collective-permute-done | bytes 24608 | tf_op jit(solution)/shard_map/ppermute | solution.py:16
  57.8 2.9 %collective-permute-done.6 = bf16[32,6,1,64]{0,3,2,1:T(8,128)(2,1)S(1)} collective-permute-done((bf16[32,6,1,64]{0,3,2,1:T(8,128)(2,1)S(1)}, bf16[32,6,1,64]{0,3,2,1:T(8,128)(2,1)S(1)}, u32[]{:S(2)}, u32[]{:S(2)}) %collective-permute-start.6) | collective-permute-done | bytes 24608 | tf_op jit(solution)/shard_map/ppermute | solution.py:14
  68.0 8.0 %all_to_all.5 = bf16[8,2,512]{2,1,0:T(2,128)(2,1)S(1)} all-to-all(bf16[8,2,512]{2,1,0:T(2,128)(2,1)S(1)} %reshape.255), channel_id=1, replica_groups=mesh['gx'=4,'gy'=8] {'gy'}, dimensions={0} | all-to-all | bytes 32768 | tf_op jit(solution)/shard_map/all_to_all | solution.py:79
  76.2 8.5 %all_gather.3 = bf16[64,8,16,4]{0,2,3,1:T(8,128)(2,1)S(1)} all-gather(bf16[64,2,16,4]{0,2,3,1:T(8,128)(2,1)S(1)} %bitcast.289), channel_id=1, replica_groups=mesh['gx'=4,'gy'=8] {'gx'}, dimensions={1}, use_global_device_ids=true | all-gather | bytes 81920 | tf_op jit(solution)/shard_map/all_gather | solution.py:81
  87.2 3.5 %collective-permute-start.9 = (bf16[64,8,16,1]{0,2,3,1:T(8,128)(2,1)S(1)}, bf16[64,8,16,1]{0,2,3,1:T(8,128)(2,1)S(1)}, u32[]{:S(2)}, u32[]{:S(2)}) collective-permute-start(bf16[64,8,16,1]{0,2,3,1:T(8,128)(2,1)S(1)} %get-tuple-element.130), channel_id=1, source_target_pairs={{1,0},{2,1},{3,2},{4,3},{5,4},{6,5},{7,6},{0,7},{9,8},{10,9},{11,1... | collective-permute-start | bytes 49160 | tf_op jit(solution)/shard_map/ppermute | solution.py:16
  90.8 1.6 %collective-permute-done.9 = bf16[64,8,16,1]{0,2,3,1:T(8,128)(2,1)S(1)} collective-permute-done((bf16[64,8,16,1]{0,2,3,1:T(8,128)(2,1)S(1)}, bf16[64,8,16,1]{0,2,3,1:T(8,128)(2,1)S(1)}, u32[]{:S(2)}, u32[]{:S(2)}) %collective-permute-start.9) | collective-permute-done | bytes 16416 | tf_op jit(solution)/shard_map/ppermute | solution.py:16
  (172 shorter events, 33.5 us)
Async XLA Ops:
  0.6 7.8 %copy-start = (bf16[32,8,8,128]{3,2,1,0:T(8,128)(2,1)S(1)}, bf16[32,8,8,128]{3,2,1,0:T(8,128)(2,1)}, u32[]{:S(2)}) copy-start(bf16[32,8,8,128]{3,2,1,0:T(8,128)(2,1)} %param.7) | copy-start | bytes 1572868
  0.6 11.5 %copy-start.2 = (bf16[27,32,32]{2,1,0:T(8,128)(2,1)S(1)}, bf16[27,32,32]{2,1,0:T(8,128)(2,1)}, u32[]{:S(2)}) copy-start(bf16[27,32,32]{2,1,0:T(8,128)(2,1)} %param.8) | copy-start | bytes 165892
  2.1 6.3 %collective-permute-start = (bf16[32,1,8,128]{3,0,2,1:T(8,128)(2,1)S(1)}, bf16[32,1,8,128]{3,0,2,1:T(8,128)(2,1)S(1)}, u32[]{:S(2)}, u32[]{:S(2)}) collective-permute-start(bf16[32,1,8,128]{3,0,2,1:T(8,128)(2,1)S(1)} %get-tuple-element.57), channel_id=1, source_target_pairs={{0,8},{8,16},{16,24},{24,0},{1,9},{9,17},{17,25},{25,1},{2,10},{10... | collective-permute-start | bytes 196616 | tf_op jit(solution)/shard_map/ppermute | solution.py:14
  5.1 4.7 %collective-permute-start.1 = (bf16[32,1,8,128]{3,0,2,1:T(8,128)(2,1)S(1)}, bf16[32,1,8,128]{3,0,2,1:T(8,128)(2,1)S(1)}, u32[]{:S(2)}, u32[]{:S(2)}) collective-permute-start(bf16[32,1,8,128]{3,0,2,1:T(8,128)(2,1)S(1)} %get-tuple-element.56), channel_id=1, source_target_pairs={{8,0},{16,8},{24,16},{0,24},{9,1},{17,9},{25,17},{1,25},{10,2},{18... | collective-permute-start | bytes 196616 | tf_op jit(solution)/shard_map/ppermute | solution.py:16
  9.9 4.3 %collective-permute-start.3 = (bf16[32,10,1,128]{3,0,2,1:T(8,128)(2,1)S(1)}, bf16[32,10,1,128]{3,0,2,1:T(8,128)(2,1)S(1)}, u32[]{:S(2)}, u32[]{:S(2)}) collective-permute-start(bf16[32,10,1,128]{3,0,2,1:T(8,128)(2,1)S(1)} %get-tuple-element.52), channel_id=1, source_target_pairs={{1,0},{2,1},{3,2},{4,3},{5,4},{6,5},{7,6},{0,7},{9,8},{10,9},{11,1... | collective-permute-start | bytes 245768 | tf_op jit(solution)/shard_map/ppermute | solution.py:16
  12.1 5.7 %collective-permute-start.2 = (bf16[32,10,1,128]{3,0,2,1:T(8,128)(2,1)S(1)}, bf16[32,10,1,128]{3,0,2,1:T(8,128)(2,1)S(1)}, u32[]{:S(2)}, u32[]{:S(2)}) collective-permute-start(bf16[32,10,1,128]{3,0,2,1:T(8,128)(2,1)S(1)} %get-tuple-element.51), channel_id=1, source_target_pairs={{0,1},{1,2},{2,3},{3,4},{4,5},{5,6},{6,7},{7,0},{8,9},{9,10},{10,1... | collective-permute-start | bytes 245768 | tf_op jit(solution)/shard_map/ppermute | solution.py:14
  37.8 1.1 %copy-start.13 = (f32[32]{0:T(128)S(1)}, f32[32]{0:T(128)}, u32[]{:S(2)}) copy-start(f32[32]{0:T(128)} %param.9) | copy-start | bytes 388
  47.3 7.9 %copy-start.3 = (bf16[27,64,32]{1,2,0:T(8,128)(2,1)S(1)}, bf16[27,64,32]{1,2,0:T(8,128)(2,1)}, u32[]{:S(2)}) copy-start(bf16[27,64,32]{1,2,0:T(8,128)(2,1)} %param.10) | copy-start | bytes 331780
  47.4 4.4 %collective-permute-start.5 = (bf16[32,1,4,64]{0,3,2,1:T(8,128)(2,1)S(1)}, bf16[32,1,4,64]{0,3,2,1:T(8,128)(2,1)S(1)}, u32[]{:S(2)}, u32[]{:S(2)}) collective-permute-start(bf16[32,1,4,64]{0,3,2,1:T(8,128)(2,1)S(1)} %get-tuple-element.99), channel_id=1, source_target_pairs={{8,0},{16,8},{24,16},{0,24},{9,1},{17,9},{25,17},{1,25},{10,2},{18... | collective-permute-start | bytes 49160 | tf_op jit(solution)/shard_map/ppermute | solution.py:16
  49.5 5.2 %collective-permute-start.4 = (bf16[32,1,4,64]{0,3,2,1:T(8,128)(2,1)S(1)}, bf16[32,1,4,64]{0,3,2,1:T(8,128)(2,1)S(1)}, u32[]{:S(2)}, u32[]{:S(2)}) collective-permute-start(bf16[32,1,4,64]{0,3,2,1:T(8,128)(2,1)S(1)} %get-tuple-element.98), channel_id=1, source_target_pairs={{0,8},{8,16},{16,24},{24,0},{1,9},{9,17},{17,25},{25,1},{2,10},{10... | collective-permute-start | bytes 49160 | tf_op jit(solution)/shard_map/ppermute | solution.py:14
  54.7 3.1 %collective-permute-start.7 = (bf16[32,6,1,64]{0,3,2,1:T(8,128)(2,1)S(1)}, bf16[32,6,1,64]{0,3,2,1:T(8,128)(2,1)S(1)}, u32[]{:S(2)}, u32[]{:S(2)}) collective-permute-start(bf16[32,6,1,64]{0,3,2,1:T(8,128)(2,1)S(1)} %get-tuple-element.76), channel_id=1, source_target_pairs={{1,0},{2,1},{3,2},{4,3},{5,4},{6,5},{7,6},{0,7},{9,8},{10,9},{11,1... | collective-permute-start | bytes 73736 | tf_op jit(solution)/shard_map/ppermute | solution.py:16
  54.8 5.9 %collective-permute-start.6 = (bf16[32,6,1,64]{0,3,2,1:T(8,128)(2,1)S(1)}, bf16[32,6,1,64]{0,3,2,1:T(8,128)(2,1)S(1)}, u32[]{:S(2)}, u32[]{:S(2)}) collective-permute-start(bf16[32,6,1,64]{0,3,2,1:T(8,128)(2,1)S(1)} %get-tuple-element.75), channel_id=1, source_target_pairs={{0,1},{1,2},{2,3},{3,4},{4,5},{5,6},{6,7},{7,0},{8,9},{9,10},{10,1... | collective-permute-start | bytes 73736 | tf_op jit(solution)/shard_map/ppermute | solution.py:14
  66.2 0.8 copy-start.11
  67.0 17.8 %copy-start.1 = (bf16[27,128,64]{1,2,0:T(8,128)(2,1)S(1)}, bf16[27,128,64]{1,2,0:T(8,128)(2,1)}, u32[]{:S(2)}) copy-start(bf16[27,128,64]{1,2,0:T(8,128)(2,1)} %param.12) | copy-start | bytes 1327108
  84.7 6.1 %collective-permute-start.8 = (bf16[64,8,16,1]{0,2,3,1:T(8,128)(2,1)S(1)}, bf16[64,8,16,1]{0,2,3,1:T(8,128)(2,1)S(1)}, u32[]{:S(2)}, u32[]{:S(2)}) collective-permute-start(bf16[64,8,16,1]{0,2,3,1:T(8,128)(2,1)S(1)} %get-tuple-element.131), channel_id=1, source_target_pairs={{0,1},{1,2},{2,3},{3,4},{4,5},{5,6},{6,7},{7,0},{8,9},{9,10},{10,1... | collective-permute-start | bytes 49160 | tf_op jit(solution)/shard_map/ppermute | solution.py:14
  87.2 5.1 %collective-permute-start.9 = (bf16[64,8,16,1]{0,2,3,1:T(8,128)(2,1)S(1)}, bf16[64,8,16,1]{0,2,3,1:T(8,128)(2,1)S(1)}, u32[]{:S(2)}, u32[]{:S(2)}) collective-permute-start(bf16[64,8,16,1]{0,2,3,1:T(8,128)(2,1)S(1)} %get-tuple-element.130), channel_id=1, source_target_pairs={{1,0},{2,1},{3,2},{4,3},{5,4},{6,5},{7,6},{0,7},{9,8},{10,9},{11,1... | collective-permute-start | bytes 49160 | tf_op jit(solution)/shard_map/ppermute | solution.py:16
  92.4 0.6 copy-start.9
  94.3 0.9 copy-start.10
  96.5 1.0 copy-start.8
  96.7 1.0 %copy-start.7 = (bf16[3,128,64]{1,2,0:T(8,128)(2,1)S(1)}, bf16[3,128,64]{1,2,0:T(8,128)(2,1)}, u32[]{:S(2)}) copy-start(bf16[3,128,64]{1,2,0:T(8,128)(2,1)} %get-tuple-element.70) | copy-start | bytes 147460
  97.0 1.0 copy-start.6
  97.1 1.0 %copy-start.5 = (bf16[3,128,64]{1,2,0:T(8,128)(2,1)S(1)}, bf16[3,128,64]{1,2,0:T(8,128)(2,1)}, u32[]{:S(2)}) copy-start(bf16[3,128,64]{1,2,0:T(8,128)(2,1)} %get-tuple-element.68) | copy-start | bytes 147460
  97.5 0.9 copy-start.4
  98.4 0.9 copy-start.12
